TPU v7x, 32 devices: a whole 2x2x4 slice. The times are simulated.
32 devices in a mesh: row: 8 (over y, x, core), col: 4 (over z).
Axes of the slice: x: 2, y: 2, z: 4, core: 2. Of those that a mesh axis runs over, the one named last changes fastest.
Arguments:
- src_points: bfloat16 [8192, 256], P('row'), may hold values from -32 to 32, as said below
- tgt_points: bfloat16 [16384, 256], P(('col', 'row')), may hold values from -32 to 32, as said below
- log_src_mass: float32 [8192], P('row'), may hold values from -3 to 3
- log_tgt_mass: float32 [16384], P('col'), may hold values from -3 to 3
Outputs:
- src_potential: float32 [8192], P('row')
- tgt_potential: float32 [16384], P('col')
- mean_potentials: float32 [], replicated
Inputs may be any that keep to these rules, and one draw needn't show every extreme that they name: `src_points`: point coordinates. `tgt_points`: point coordinates.
All inputs are finite; a program needn't handle non-finite values.
Results may differ from a plain program's by a relative error of at most 0.0003.
Values may be sent and summed in bfloat16 or wider, within the bound.
A program may use at most 64 MiB of HBM per device.

v0:
```python
import jax
import jax.numpy as jnp
from jax import lax
from jax.sharding import PartitionSpec as P

ITERS = 3
entropy_weight = 0.1


def combined_all(value, axis, combine):
    everything = jax.tree.map(lambda part: lax.all_gather(part, axis), value)
    leading = jax.tree.map(lambda part: part[0], everything)

    def turn(k, so_far):
        return combine(so_far, jax.tree.map(lambda part: part[k], everything))

    return lax.fori_loop(1, lax.axis_size(axis), turn, leading)


def cost_block(points_a, squares_a, points_b, squares_b):
    product = lax.dot_general(
        points_a, points_b, (((1,), (1,)), ((), ())), preferred_element_type=jnp.float32
    )
    return (squares_a[:, None] + squares_b[None, :] - 2.0 * product) / points_a.shape[1]


def combine(early, later):
    top = jnp.maximum(early[0], later[0])
    return (top, early[1] * jnp.exp(early[0] - top) + later[1] * jnp.exp(later[0] - top))


def body(src_points, tgt_points, log_src_mass, log_tgt_mass):
    targets = lax.all_gather(tgt_points, "row", axis=0, tiled=True)
    sqy = jnp.sum(targets.astype(jnp.float32) ** 2, axis=1)
    count = src_points.shape[0]
    block = min(256, count)
    blocks = count // block
    src_blocks = src_points.reshape(blocks, block, -1)
    sq_blocks = jnp.sum(src_points.astype(jnp.float32) ** 2, axis=1).reshape(blocks, block)
    mass_blocks = log_src_mass.reshape(blocks, block)
    width_tgt = targets.shape[0]
    tgt_potential = jnp.zeros((width_tgt,), jnp.float32)
    src_potential = jnp.zeros((count,), jnp.float32)
    for step in range(ITERS):

        def row_terms(points, squares):
            cost = cost_block(points, squares, targets, sqy)
            return log_tgt_mass[None, :] + (tgt_potential[None, :] - cost) / entropy_weight

        def row_pair(item):
            terms = row_terms(item[0], item[1])
            top = jnp.max(terms, axis=1)
            return (top, jnp.sum(jnp.exp(terms - top[:, None]), axis=1))

        top, total = lax.map(row_pair, (src_blocks, sq_blocks))
        top, total = combined_all((top.reshape(-1), total.reshape(-1)), "col", combine)
        src_potential = -entropy_weight * (top + jnp.log(total))
        pot_blocks = src_potential.reshape(blocks, block)

        def col_terms(points, squares, mass, pot):
            cost = cost_block(points, squares, targets, sqy)
            return mass[:, None] + (pot[:, None] - cost) / entropy_weight

        def pair_step(carry, item):
            terms = col_terms(item[0], item[1], item[2], item[3])
            block_top = jnp.max(terms, axis=0)
            block_sum = jnp.sum(jnp.exp(terms - block_top[None, :]), axis=0)
            return (combine(carry, (block_top, block_sum)), None)

        start = (
            jnp.full((width_tgt,), -jnp.inf, jnp.float32),
            jnp.zeros((width_tgt,), jnp.float32),
        )
        inputs = (src_blocks, sq_blocks, mass_blocks, pot_blocks)
        (top, total), unused = lax.scan(pair_step, start, inputs)
        top, total = combined_all((top, total), "row", combine)
        tgt_potential = -entropy_weight * (top + jnp.log(total))
    sources_all = count * lax.axis_size("row")
    targets_all = width_tgt * lax.axis_size("col")
    local = jnp.sum(src_potential) / (sources_all * lax.axis_size("col")) + jnp.sum(
        tgt_potential
    ) / (targets_all * lax.axis_size("row"))
    mean_potentials = lax.psum(local, ("row", "col"))
    return (src_potential, tgt_potential, mean_potentials)


def solution(mesh):
    return jax.shard_map(
        body,
        mesh=mesh,
        in_specs=(P("row", None), P(("col", "row"), None), P("row"), P("col")),
        out_specs=(P("row"), P("col"), P()),
        check_vma=False,
    )
```

profile of v0, /device:TPU:0, one launch (start us, length us, event | category | flops | bytes accessed | tf_op | source)
XLA Modules:
  0.0 320.3 jit_solution(3803695196308315043)
XLA Ops:
  7.2 0.7 all-gather.14.cloned.1.call-update
  8.0 1.3 multiply_reduce_fusion.1
  9.2 0.7 reshape.65
  9.9 30.5 %all-gather.14.cloned.1.call-done = bf16[4096,256]{1,0:T(8,128)(2,1)} async-done(((bf16[512,256]{1,0:T(8,128)(2,1)}), bf16[4096,256]{1,0:T(8,128)(2,1)}) %all-gather.14.cloned.1.call-update) | async-done | bytes 2097168 | tf_op jit(solution)/shard_map/all_gather | solution.py:33
  40.4 2.2 multiply_reduce_fusion
  42.6 15.6 %while.177 = (s32[]{:T(128)}, f32[4,256]{1,0:T(4,128)S(1)}, f32[4,256]{1,0:T(4,128)S(1)}, f32[4096]{0:T(1024)}, f32[4,256]{1,0:T(4,128)S(1)}, /*index=5*/f32[409...) while((s32[]{:T(128)}, f32[4,256]{1,0:T(4,128)S(1)}, ...), condition=%wide.region_5.6_spmd, body=%wide.region_2.5_spmd.sunk | while | flops 547356160 | bytes 10660465 | solution.py:55
  42.7 3.1 fusion.81
  45.7 0.7 exponential_reduce_fusion.12
  46.6 3.1 fusion.81
  49.6 0.7 exponential_reduce_fusion.12
  50.5 3.1 fusion.81
  53.5 0.7 exponential_reduce_fusion.12
  54.4 3.1 fusion.81
  57.4 0.7 exponential_reduce_fusion.12
  58.3 13.3 %all-gather.6 = f32[4,1,1024]{2,1,0:T(1,128)S(1)} all-gather(f32[1,1,1024]{2,1,0:T(1,128)S(1)} %reshape.89), channel_id=1, replica_groups=mesh['row'=8,'col'=4] {'col'}, dimensions={0}, use_global_device_ids=true | all-gather | bytes 20480 | tf_op jit(solution)/shard_map/all_gather | solution.py:11
  71.5 13.2 %all-gather.7 = f32[4,1,1024]{2,1,0:T(1,128)S(1)} all-gather(f32[1,1,1024]{2,1,0:T(1,128)S(1)} %reshape.91), channel_id=1, replica_groups=mesh['row'=8,'col'=4] {'col'}, dimensions={0}, use_global_device_ids=true | all-gather | bytes 20480 | tf_op jit(solution)/shard_map/all_gather | solution.py:11
  85.0 15.2 %while.186 = (s32[]{:T(128)}, f32[4096]{0:T(1024)S(1)}, f32[4096]{0:T(1024)S(1)}, f32[4,256]{1,0:T(4,128)S(1)}, f32[4,256]{1,0:T(4,128)S(1)}, /*index=5*/f32[4,2...) while((s32[]{:T(128)}, f32[4096]{0:T(1024)S(1)}, ...), condition=%wide.region_11.12_spmd.clone, body=%wide.region_8.11_spmd.clone.sunk | while | flops 547381248 | bytes 10790527 | solution.py:75
  85.0 3.1 fusion.87
  88.8 3.1 fusion.87
  92.6 3.1 fusion.87
  95.8 0.6 exponential_reduce_fusion.15
  96.4 3.1 fusion.87
  100.2 9.2 %all-gather = f32[32768]{0:T(1024)S(1)} all-gather(f32[4096]{0:T(1024)S(1)} %get-tuple-element.1088), channel_id=2, replica_groups=mesh['row'=8,'col'=4] {'row'}, dimensions={0}, use_global_device_ids=true | all-gather | bytes 147456 | tf_op jit(solution)/shard_map/all_gather | solution.py:11
  109.4 8.3 %all-gather.1 = f32[32768]{0:T(1024)S(1)} all-gather(f32[4096]{0:T(1024)S(1)} %get-tuple-element.1089), channel_id=3, replica_groups=mesh['row'=8,'col'=4] {'row'}, dimensions={0}, use_global_device_ids=true | all-gather | bytes 147456 | tf_op jit(solution)/shard_map/all_gather | solution.py:11
  118.3 16.0 %while.180 = (s32[]{:T(128)}, f32[4,256]{1,0:T(4,128)S(1)}, f32[4,256]{1,0:T(4,128)S(1)}, f32[4096]{0:T(1024)S(1)}, f32[4096]{0:T(1024)S(1)}, /*index=5*/f32[4,2...) while((s32[]{:T(128)}, f32[4,256]{1,0:T(4,128)S(1)}, ...), condition=%wide.region_17.18_spmd, body=%wide.region_14.17_spmd.sunk | while | flops 547356160 | bytes 10676857 | solution.py:55
  118.4 3.2 fusion.83
  121.5 0.7 exponential_reduce_fusion.13
  122.4 3.2 fusion.83
  125.5 0.7 exponential_reduce_fusion.13
  126.4 3.2 fusion.83
  129.5 0.7 exponential_reduce_fusion.13
  130.4 3.2 fusion.83
  133.5 0.7 exponential_reduce_fusion.13
  134.4 13.2 %all-gather.8 = f32[4,1,1024]{2,1,0:T(1,128)S(1)} all-gather(f32[1,1,1024]{2,1,0:T(1,128)S(1)} %reshape.93), channel_id=1, replica_groups=mesh['row'=8,'col'=4] {'col'}, dimensions={0}, use_global_device_ids=true | all-gather | bytes 20480 | tf_op jit(solution)/shard_map/all_gather | solution.py:11
  147.6 13.2 %all-gather.9 = f32[4,1,1024]{2,1,0:T(1,128)S(1)} all-gather(f32[1,1,1024]{2,1,0:T(1,128)S(1)} %reshape.95), channel_id=1, replica_groups=mesh['row'=8,'col'=4] {'col'}, dimensions={0}, use_global_device_ids=true | all-gather | bytes 20480 | tf_op jit(solution)/shard_map/all_gather | solution.py:11
  161.0 15.2 %while.187 = (s32[]{:T(128)}, f32[4096]{0:T(1024)S(1)}, f32[4096]{0:T(1024)S(1)}, f32[4,256]{1,0:T(4,128)S(1)}, f32[4,256]{1,0:T(4,128)S(1)}, /*index=5*/f32[4,2...) while((s32[]{:T(128)}, f32[4096]{0:T(1024)S(1)}, ...), condition=%wide.region_23.24_spmd.clone, body=%wide.region_20.23_spmd.clone.sunk | while | flops 547381248 | bytes 10790527 | solution.py:75
  161.1 3.1 fusion.90
  164.2 0.6 exponential_reduce_fusion.16
  164.9 3.1 fusion.90
  168.7 3.1 fusion.90
  172.5 3.1 fusion.90
  176.2 9.3 %all-gather.2 = f32[32768]{0:T(1024)S(1)} all-gather(f32[4096]{0:T(1024)S(1)} %get-tuple-element.1096), channel_id=4, replica_groups=mesh['row'=8,'col'=4] {'row'}, dimensions={0}, use_global_device_ids=true | all-gather | bytes 147456 | tf_op jit(solution)/shard_map/all_gather | solution.py:11
  185.6 8.3 %all-gather.3 = f32[32768]{0:T(1024)S(1)} all-gather(f32[4096]{0:T(1024)S(1)} %get-tuple-element.1097), channel_id=5, replica_groups=mesh['row'=8,'col'=4] {'row'}, dimensions={0}, use_global_device_ids=true | all-gather | bytes 147456 | tf_op jit(solution)/shard_map/all_gather | solution.py:11
  194.5 16.0 %while.183 = (s32[]{:T(128)}, f32[4,256]{1,0:T(4,128)S(1)}, f32[4,256]{1,0:T(4,128)S(1)}, f32[4096]{0:T(1024)S(1)}, f32[4096]{0:T(1024)S(1)}, /*index=5*/f32[4,2...) while((s32[]{:T(128)}, f32[4,256]{1,0:T(4,128)S(1)}, ...), condition=%wide.region_29.30_spmd, body=%wide.region_26.29_spmd.sunk | while | flops 547356160 | bytes 10676857 | solution.py:55
  194.6 3.2 fusion.85
  197.7 0.7 exponential_reduce_fusion.14
  198.6 3.2 fusion.85
  201.7 0.7 exponential_reduce_fusion.14
  202.6 3.2 fusion.85
  205.7 0.7 exponential_reduce_fusion.14
  206.6 3.2 fusion.85
  209.7 0.7 exponential_reduce_fusion.14
  210.6 13.2 %all-gather.10 = f32[4,1,1024]{2,1,0:T(1,128)S(1)} all-gather(f32[1,1,1024]{2,1,0:T(1,128)S(1)} %reshape.97), channel_id=1, replica_groups=mesh['row'=8,'col'=4] {'col'}, dimensions={0}, use_global_device_ids=true | all-gather | bytes 20480 | tf_op jit(solution)/shard_map/all_gather | solution.py:11
  223.8 13.2 %all-gather.11 = f32[4,1,1024]{2,1,0:T(1,128)S(1)} all-gather(f32[1,1,1024]{2,1,0:T(1,128)S(1)} %reshape.99), channel_id=1, replica_groups=mesh['row'=8,'col'=4] {'col'}, dimensions={0}, use_global_device_ids=true | all-gather | bytes 20480 | tf_op jit(solution)/shard_map/all_gather | solution.py:11
  237.2 0.6 fusion.52
  238.4 15.2 %while.188 = (s32[]{:T(128)}, f32[4096]{0:T(1024)S(1)}, f32[4096]{0:T(1024)S(1)}, f32[4,256]{1,0:T(4,128)S(1)}, f32[4,256]{1,0:T(4,128)S(1)}, /*index=5*/f32[4,2...) while((s32[]{:T(128)}, f32[4096]{0:T(1024)S(1)}, ...), condition=%wide.region_35.36_spmd.clone, body=%wide.region_32.35_spmd.clone.sunk | while | flops 547381248 | bytes 10790527 | solution.py:75
  238.4 3.1 fusion.93
  242.2 3.1 fusion.93
  246.0 3.1 fusion.93
  249.8 3.1 fusion.93
  253.6 9.2 %all-gather.4 = f32[32768]{0:T(1024)S(1)} all-gather(f32[4096]{0:T(1024)S(1)} %get-tuple-element.1104), channel_id=6, replica_groups=mesh['row'=8,'col'=4] {'row'}, dimensions={0}, use_global_device_ids=true | all-gather | bytes 147456 | tf_op jit(solution)/shard_map/all_gather | solution.py:11
  262.8 8.3 %all-gather.5 = f32[32768]{0:T(1024)S(1)} all-gather(f32[4096]{0:T(1024)S(1)} %get-tuple-element.1105), channel_id=7, replica_groups=mesh['row'=8,'col'=4] {'row'}, dimensions={0}, use_global_device_ids=true | all-gather | bytes 147456 | tf_op jit(solution)/shard_map/all_gather | solution.py:11
  271.7 1.3 fusion.51
  274.3 39.1 %psum.7 = f32[]{:T(128)} all-reduce(f32[]{:T(128)S(6)} %add.464), channel_id=1, replica_groups=mesh['row'=8,'col'=4] {'row','col'}, use_global_device_ids=true, to_apply=%region_40.41 | all-reduce | flops 1 | bytes 8 | tf_op jit(solution)/shard_map/psum | solution.py:83
  (203 shorter events, 12.0 us)
Async XLA Ops:
  7.2 33.2 %all-gather.14.cloned.1.call-start = ((), (), s32[]{:S(2)}) async-start(), calls=%async_computation | async-start | bytes 2359296 | tf_op jit(solution)/shard_map/all_gather | solution.py:33
  85.0 33.3 %copy-start.1 = (f32[4096]{0:T(1024)S(1)}, f32[4096]{0:T(1024)}, u32[]{:S(2)}) copy-start(f32[4096]{0:T(1024)} %get-tuple-element.2387) | copy-start | bytes 49156
  237.8 0.6 copy-start
Sparse Core Ops, SparseCore 0:
  9.9 30.4 all-gather.13
where the time goes:
time: 322 us; the launch traced here: 320 us
  blocking collectives  171 us (53%)
  matrix products  75.1 us (23%)
  waiting for transfers between devices  31.2 us (10%)
  other arithmetic  22 us (7%)
  between operations  15.7 us (5%)
  local copies, waits for them, and re-layouts  3.61 us (1%)
    all_gather x12, blocking collectives, combined_all(): everything = jax.tree.map(lambda part: lax.all_gather(part, axis), value)  132 us
    dot_general x24, matrix products, cost_block(): lax.dot_general(points_a, points_b, (((1,), (1,)), ((), ())), preferred_e...  75.1 us
    psum x1, blocking collectives, body(): mean_potentials = lax.psum(local, ('row', 'col'))  39.1 us
    all_gather x1, waiting for transfers between devices, body(): targets = lax.all_gather(tgt_points, 'row', axis=0, tiled=True)  30.5 us
    reduce_sum x12, other arithmetic, row_pair(): return (top, jnp.sum(jnp.exp(terms - top[:, None]), axis=1))  8.61 us
    reduce_sum x12, other arithmetic, pair_step(): block_sum = jnp.sum(jnp.exp(terms - block_top[None, :]), axis=0)  7.15 us
  transfers between devices with their start and end apart: 1, of which 1 were waited for; matrix products, arithmetic and copies ran while one was open for 1% of the time, Pallas kernels for 0%

commit v1 on v0

--- a/solution.py
+++ b/solution.py
@@ -30,7 +30,12 @@
 
 
 def body(src_points, tgt_points, log_src_mass, log_tgt_mass):
-    targets = lax.all_gather(tgt_points, "row", axis=0, tiled=True)
+    ring = [tgt_points]
+    for hop in range(7):
+        ring.append(lax.ppermute(ring[-1], "row", [(dev, (dev + 1) % 8) for dev in range(8)]))
+    targets = jnp.roll(
+        jnp.concatenate(ring[::-1], axis=0), (lax.axis_index("row") + 1) * ring[0].shape[0], axis=0
+    )
     sqy = jnp.sum(targets.astype(jnp.float32) ** 2, axis=1)
     count = src_points.shape[0]
     block = min(256, count)

time: 322 us -> 282 us (0.88)
  matrix products: 75.1 us -> 35.4 us
  waiting for transfers between devices: 31.2 us -> 45.3 us
  between operations: 15.7 us -> 2.5 us
    ppermute x0 -> x7, waiting for transfers between devices: none -> 45.3 us  [body(): lax.ppermute(ring[-1], 'row', [(dev, (dev + 1) % 8) for dev in range(8)])]
    dot_general x24, matrix products: 75.1 us -> 35.4 us  [cost_block(): lax.dot_general(points_a, points_b, (((1,), (1,)), ((), ())), preferred_e...]
    all_gather x1 -> x0, waiting for transfers between devices: 30.5 us -> none  [body(): targets = lax.all_gather(tgt_points, 'row', axis=0, tiled=True)]
  transfers between devices with their start and end apart: 1 -> 7, of which waited for: 1 -> 7; matrix products, arithmetic and copies ran while one was open for 1% -> 1% of each run, Pallas kernels for 0% -> 0%
where the time goes in v1:
time: 282 us
  blocking collectives  172 us (61%)
  waiting for transfers between devices  45.3 us (16%)
  matrix products  35.4 us (13%)
  other arithmetic  20.4 us (7%)
  local copies, waits for them, and re-layouts  4.07 us (1%)
    all_gather x12, blocking collectives, combined_all(): everything = jax.tree.map(lambda part: lax.all_gather(part, axis), value)  133 us
    ppermute x7, waiting for transfers between devices, body(): lax.ppermute(ring[-1], 'row', [(dev, (dev + 1) % 8) for dev in range(8)])  45.3 us
    psum x1, blocking collectives, body(): mean_potentials = lax.psum(local, ('row', 'col'))  39.3 us
    dot_general x24, matrix products, cost_block(): lax.dot_general(points_a, points_b, (((1,), (1,)), ((), ())), preferred_e...  35.4 us
    reduce_sum x12, other arithmetic, row_pair(): return (top, jnp.sum(jnp.exp(terms - top[:, None]), axis=1))  8.61 us
    reduce_sum x12, other arithmetic, pair_step(): block_sum = jnp.sum(jnp.exp(terms - block_top[None, :]), axis=0)  7.15 us
  transfers between devices with their start and end apart: 7, of which 7 were waited for; matrix products, arithmetic and copies ran while one was open for 1% of the time, Pallas kernels for 0%

profile of v1, /device:TPU:0, one launch (start us, length us, event | category | flops | bytes accessed | tf_op | source)
XLA Modules:
  0.0 282.0 jit_solution(7732518427664228320)
XLA Ops:
  1.2 7.1 %collective-permute-done = bf16[512,256]{1,0:T(8,128)(2,1)S(1)} collective-permute-done((bf16[512,256]{1,0:T(8,128)(2,1)}, bf16[512,256]{1,0:T(8,128)(2,1)S(1)}, u32[]{:S(2)}, u32[]{:S(2)}) %collective-permute-start) | collective-permute-done | bytes 262176 | tf_op jit(solution)/shard_map/ppermute | solution.py:35
  8.3 6.7 %collective-permute-done.1 = bf16[512,256]{1,0:T(8,128)(2,1)S(1)} collective-permute-done((bf16[512,256]{1,0:T(8,128)(2,1)S(1)}, bf16[512,256]{1,0:T(8,128)(2,1)S(1)}, u32[]{:S(2)}, u32[]{:S(2)}) %collective-permute-start.1) | collective-permute-done | bytes 262176 | tf_op jit(solution)/shard_map/ppermute | solution.py:35
  15.0 6.7 %collective-permute-done.2 = bf16[512,256]{1,0:T(8,128)(2,1)S(1)} collective-permute-done((bf16[512,256]{1,0:T(8,128)(2,1)S(1)}, bf16[512,256]{1,0:T(8,128)(2,1)S(1)}, u32[]{:S(2)}, u32[]{:S(2)}) %collective-permute-start.2) | collective-permute-done | bytes 262176 | tf_op jit(solution)/shard_map/ppermute | solution.py:35
  21.7 6.7 %collective-permute-done.3 = bf16[512,256]{1,0:T(8,128)(2,1)S(1)} collective-permute-done((bf16[512,256]{1,0:T(8,128)(2,1)S(1)}, bf16[512,256]{1,0:T(8,128)(2,1)S(1)}, u32[]{:S(2)}, u32[]{:S(2)}) %collective-permute-start.3) | collective-permute-done | bytes 262176 | tf_op jit(solution)/shard_map/ppermute | solution.py:35
  28.4 6.7 %collective-permute-done.4 = bf16[512,256]{1,0:T(8,128)(2,1)S(1)} collective-permute-done((bf16[512,256]{1,0:T(8,128)(2,1)S(1)}, bf16[512,256]{1,0:T(8,128)(2,1)S(1)}, u32[]{:S(2)}, u32[]{:S(2)}) %collective-permute-start.4) | collective-permute-done | bytes 262176 | tf_op jit(solution)/shard_map/ppermute | solution.py:35
  35.1 6.7 %collective-permute-done.5 = bf16[512,256]{1,0:T(8,128)(2,1)S(1)} collective-permute-done((bf16[512,256]{1,0:T(8,128)(2,1)S(1)}, bf16[512,256]{1,0:T(8,128)(2,1)S(1)}, u32[]{:S(2)}, u32[]{:S(2)}) %collective-permute-start.5) | collective-permute-done | bytes 262176 | tf_op jit(solution)/shard_map/ppermute | solution.py:35
  41.9 1.3 multiply_reduce_fusion.1
  43.8 4.7 %collective-permute-done.6 = bf16[512,256]{1,0:T(8,128)(2,1)S(1)} collective-permute-done((bf16[512,256]{1,0:T(8,128)(2,1)S(1)}, bf16[512,256]{1,0:T(8,128)(2,1)S(1)}, u32[]{:S(2)}, u32[]{:S(2)}) %collective-permute-start.6) | collective-permute-done | bytes 262176 | tf_op jit(solution)/shard_map/ppermute | solution.py:35
  49.8 9.3 %while.177 = (s32[]{:T(128)}, f32[4,256]{1,0:T(4,128)S(1)}, f32[4,256]{1,0:T(4,128)S(1)}, f32[4096]{0:T(1024)S(1)}, f32[4,256]{1,0:T(4,128)S(1)}, /*index=5*/f32...) while((s32[]{:T(128)}, f32[4,256]{1,0:T(4,128)S(1)}, ...), condition=%wide.region_5.6_spmd, body=%wide.region_2.5_spmd.sunk | while | flops 547356160 | bytes 10659957 | solution.py:60
  49.8 1.5 fusion.81
  51.3 0.7 exponential_reduce_fusion.12
  52.1 1.5 fusion.81
  53.6 0.7 exponential_reduce_fusion.12
  54.4 1.5 fusion.81
  55.9 0.7 exponential_reduce_fusion.12
  56.8 1.5 fusion.81
  58.3 0.7 exponential_reduce_fusion.12
  59.1 14.2 %all-gather.6 = f32[4,1,1024]{2,1,0:T(1,128)S(1)} all-gather(f32[1,1,1024]{2,1,0:T(1,128)S(1)} %reshape.89), channel_id=1, replica_groups=mesh['row'=8,'col'=4] {'col'}, dimensions={0}, use_global_device_ids=true | all-gather | bytes 20480 | tf_op jit(solution)/shard_map/all_gather | solution.py:11
  73.3 13.2 %all-gather.7 = f32[4,1,1024]{2,1,0:T(1,128)S(1)} all-gather(f32[1,1,1024]{2,1,0:T(1,128)S(1)} %reshape.91), channel_id=1, replica_groups=mesh['row'=8,'col'=4] {'col'}, dimensions={0}, use_global_device_ids=true | all-gather | bytes 20480 | tf_op jit(solution)/shard_map/all_gather | solution.py:11
  86.7 8.5 %while.186 = (s32[]{:T(128)}, f32[4096]{0:T(1024)S(1)}, f32[4096]{0:T(1024)S(1)}, f32[4,256]{1,0:T(4,128)S(1)}, f32[4,256]{1,0:T(4,128)S(1)}, /*index=5*/f32[4,2...) while((s32[]{:T(128)}, f32[4096]{0:T(1024)S(1)}, ...), condition=%wide.region_11.12_spmd.clone, body=%wide.region_8.11_spmd.clone.sunk | while | flops 547381248 | bytes 10790019 | solution.py:80
  86.8 1.4 fusion.87
  88.9 1.4 fusion.87
  91.0 1.4 fusion.87
  93.1 1.4 fusion.87
  95.2 9.2 %all-gather = f32[32768]{0:T(1024)S(1)} all-gather(f32[4096]{0:T(1024)S(1)} %get-tuple-element.1088), channel_id=2, replica_groups=mesh['row'=8,'col'=4] {'row'}, dimensions={0}, use_global_device_ids=true | all-gather | bytes 147456 | tf_op jit(solution)/shard_map/all_gather | solution.py:11
  104.5 8.2 %all-gather.1 = f32[32768]{0:T(1024)S(1)} all-gather(f32[4096]{0:T(1024)S(1)} %get-tuple-element.1089), channel_id=3, replica_groups=mesh['row'=8,'col'=4] {'row'}, dimensions={0}, use_global_device_ids=true | all-gather | bytes 147456 | tf_op jit(solution)/shard_map/all_gather | solution.py:11
  113.3 9.4 %while.180 = (s32[]{:T(128)}, f32[4,256]{1,0:T(4,128)S(1)}, f32[4,256]{1,0:T(4,128)S(1)}, f32[4096]{0:T(1024)S(1)}, f32[4096]{0:T(1024)S(1)}, /*index=5*/f32[4,2...) while((s32[]{:T(128)}, f32[4,256]{1,0:T(4,128)S(1)}, ...), condition=%wide.region_17.18_spmd, body=%wide.region_14.17_spmd.sunk | while | flops 547356160 | bytes 10676349 | solution.py:60
  113.4 1.5 fusion.83
  114.9 0.7 exponential_reduce_fusion.13
  115.7 1.5 fusion.83
  117.2 0.7 exponential_reduce_fusion.13
  118.0 1.5 fusion.83
  119.5 0.7 exponential_reduce_fusion.13
  120.4 1.5 fusion.83
  121.9 0.7 exponential_reduce_fusion.13
  122.7 13.2 %all-gather.8 = f32[4,1,1024]{2,1,0:T(1,128)S(1)} all-gather(f32[1,1,1024]{2,1,0:T(1,128)S(1)} %reshape.93), channel_id=1, replica_groups=mesh['row'=8,'col'=4] {'col'}, dimensions={0}, use_global_device_ids=true | all-gather | bytes 20480 | tf_op jit(solution)/shard_map/all_gather | solution.py:11
  136.0 13.4 %all-gather.9 = f32[4,1,1024]{2,1,0:T(1,128)S(1)} all-gather(f32[1,1,1024]{2,1,0:T(1,128)S(1)} %reshape.95), channel_id=1, replica_groups=mesh['row'=8,'col'=4] {'col'}, dimensions={0}, use_global_device_ids=true | all-gather | bytes 20480 | tf_op jit(solution)/shard_map/all_gather | solution.py:11
  149.6 8.5 %while.187 = (s32[]{:T(128)}, f32[4096]{0:T(1024)S(1)}, f32[4096]{0:T(1024)S(1)}, f32[4,256]{1,0:T(4,128)S(1)}, f32[4,256]{1,0:T(4,128)S(1)}, /*index=5*/f32[4,2...) while((s32[]{:T(128)}, f32[4096]{0:T(1024)S(1)}, ...), condition=%wide.region_23.24_spmd.clone, body=%wide.region_20.23_spmd.clone.sunk | while | flops 547381248 | bytes 10790019 | solution.py:80
  149.6 1.4 fusion.90
  151.7 1.4 fusion.90
  153.8 1.4 fusion.90
  156.0 1.4 fusion.90
  158.0 9.2 %all-gather.2 = f32[32768]{0:T(1024)S(1)} all-gather(f32[4096]{0:T(1024)S(1)} %get-tuple-element.1096), channel_id=4, replica_groups=mesh['row'=8,'col'=4] {'row'}, dimensions={0}, use_global_device_ids=true | all-gather | bytes 147456 | tf_op jit(solution)/shard_map/all_gather | solution.py:11
  167.3 8.2 %all-gather.3 = f32[32768]{0:T(1024)S(1)} all-gather(f32[4096]{0:T(1024)S(1)} %get-tuple-element.1097), channel_id=5, replica_groups=mesh['row'=8,'col'=4] {'row'}, dimensions={0}, use_global_device_ids=true | all-gather | bytes 147456 | tf_op jit(solution)/shard_map/all_gather | solution.py:11
  176.2 9.4 %while.183 = (s32[]{:T(128)}, f32[4,256]{1,0:T(4,128)S(1)}, f32[4,256]{1,0:T(4,128)S(1)}, f32[4096]{0:T(1024)S(1)}, f32[4096]{0:T(1024)S(1)}, /*index=5*/f32[4,2...) while((s32[]{:T(128)}, f32[4,256]{1,0:T(4,128)S(1)}, ...), condition=%wide.region_29.30_spmd, body=%wide.region_26.29_spmd.sunk | while | flops 547356160 | bytes 10676349 | solution.py:60
  176.2 1.5 fusion.85
  177.7 0.7 exponential_reduce_fusion.14
  178.5 1.5 fusion.85
  180.1 0.7 exponential_reduce_fusion.14
  180.9 1.5 fusion.85
  182.4 0.7 exponential_reduce_fusion.14
  183.2 1.5 fusion.85
  184.8 0.7 exponential_reduce_fusion.14
  185.6 13.2 %all-gather.10 = f32[4,1,1024]{2,1,0:T(1,128)S(1)} all-gather(f32[1,1,1024]{2,1,0:T(1,128)S(1)} %reshape.97), channel_id=1, replica_groups=mesh['row'=8,'col'=4] {'col'}, dimensions={0}, use_global_device_ids=true | all-gather | bytes 20480 | tf_op jit(solution)/shard_map/all_gather | solution.py:11
  198.8 13.2 %all-gather.11 = f32[4,1,1024]{2,1,0:T(1,128)S(1)} all-gather(f32[1,1,1024]{2,1,0:T(1,128)S(1)} %reshape.99), channel_id=1, replica_groups=mesh['row'=8,'col'=4] {'col'}, dimensions={0}, use_global_device_ids=true | all-gather | bytes 20480 | tf_op jit(solution)/shard_map/all_gather | solution.py:11
  213.4 8.4 %while.188 = (s32[]{:T(128)}, f32[4096]{0:T(1024)S(1)}, f32[4096]{0:T(1024)S(1)}, f32[4,256]{1,0:T(4,128)S(1)}, f32[4,256]{1,0:T(4,128)S(1)}, /*index=5*/f32[4,2...) while((s32[]{:T(128)}, f32[4096]{0:T(1024)S(1)}, ...), condition=%wide.region_35.36_spmd.clone, body=%wide.region_32.35_spmd.clone.sunk | while | flops 547381248 | bytes 10790019 | solution.py:80
  213.4 1.4 fusion.93
  215.6 1.4 fusion.93
  217.7 1.4 fusion.93
  219.8 1.4 fusion.93
  221.9 9.2 %all-gather.4 = f32[32768]{0:T(1024)S(1)} all-gather(f32[4096]{0:T(1024)S(1)} %get-tuple-element.1104), channel_id=6, replica_groups=mesh['row'=8,'col'=4] {'row'}, dimensions={0}, use_global_device_ids=true | all-gather | bytes 147456 | tf_op jit(solution)/shard_map/all_gather | solution.py:11
  231.2 8.2 %all-gather.5 = f32[32768]{0:T(1024)S(1)} all-gather(f32[4096]{0:T(1024)S(1)} %get-tuple-element.1105), channel_id=7, replica_groups=mesh['row'=8,'col'=4] {'row'}, dimensions={0}, use_global_device_ids=true | all-gather | bytes 147456 | tf_op jit(solution)/shard_map/all_gather | solution.py:11
  240.0 1.3 fusion.51
  242.6 39.3 %psum.7 = f32[]{:T(128)} all-reduce(f32[]{:T(128)S(6)} %add.480), channel_id=1, replica_groups=mesh['row'=8,'col'=4] {'row','col'}, use_global_device_ids=true, to_apply=%region_40.41 | all-reduce | flops 1 | bytes 8 | tf_op jit(solution)/shard_map/psum | solution.py:88
  (234 shorter events, 16.1 us)
Async XLA Ops:
  0.6 48.1 %copy-start = (bf16[512,256]{1,0:T(8,128)(2,1)S(1)}, bf16[512,256]{1,0:T(8,128)(2,1)}, u32[]{:S(2)}) copy-start(bf16[512,256]{1,0:T(8,128)(2,1)} %param.29) | copy-start | bytes 786436
  0.6 7.7 %collective-permute-start = (bf16[512,256]{1,0:T(8,128)(2,1)}, bf16[512,256]{1,0:T(8,128)(2,1)S(1)}, u32[]{:S(2)}, u32[]{:S(2)}) collective-permute-start(bf16[512,256]{1,0:T(8,128)(2,1)} %param.29), channel_id=1, source_target_pairs={{0,4},{4,8},{8,12},{12,16},{16,20},{20,24},{24,28},{28,0},{1,5},{5... | collective-permute-start | bytes 786440 | tf_op jit(solution)/shard_map/ppermute | solution.py:35
  8.3 6.7 %collective-permute-start.1 = (bf16[512,256]{1,0:T(8,128)(2,1)S(1)}, bf16[512,256]{1,0:T(8,128)(2,1)S(1)}, u32[]{:S(2)}, u32[]{:S(2)}) collective-permute-start(bf16[512,256]{1,0:T(8,128)(2,1)S(1)} %collective-permute-done), channel_id=1, source_target_pairs={{0,4},{4,8},{8,12},{12,16},{16,20},{20,24},{24,28},{28,0},{1,5},{5... | collective-permute-start | bytes 786440 | tf_op jit(solution)/shard_map/ppermute | solution.py:35
  15.0 6.7 %collective-permute-start.2 = (bf16[512,256]{1,0:T(8,128)(2,1)S(1)}, bf16[512,256]{1,0:T(8,128)(2,1)S(1)}, u32[]{:S(2)}, u32[]{:S(2)}) collective-permute-start(bf16[512,256]{1,0:T(8,128)(2,1)S(1)} %collective-permute-done.1), channel_id=1, source_target_pairs={{0,4},{4,8},{8,12},{12,16},{16,20},{20,24},{24,28},{28,0},{1,5},{5... | collective-permute-start | bytes 786440 | tf_op jit(solution)/shard_map/ppermute | solution.py:35
  21.7 6.7 %collective-permute-start.3 = (bf16[512,256]{1,0:T(8,128)(2,1)S(1)}, bf16[512,256]{1,0:T(8,128)(2,1)S(1)}, u32[]{:S(2)}, u32[]{:S(2)}) collective-permute-start(bf16[512,256]{1,0:T(8,128)(2,1)S(1)} %collective-permute-done.2), channel_id=1, source_target_pairs={{0,4},{4,8},{8,12},{12,16},{16,20},{20,24},{24,28},{28,0},{1,5},{5... | collective-permute-start | bytes 786440 | tf_op jit(solution)/shard_map/ppermute | solution.py:35
  28.4 6.7 %collective-permute-start.4 = (bf16[512,256]{1,0:T(8,128)(2,1)S(1)}, bf16[512,256]{1,0:T(8,128)(2,1)S(1)}, u32[]{:S(2)}, u32[]{:S(2)}) collective-permute-start(bf16[512,256]{1,0:T(8,128)(2,1)S(1)} %collective-permute-done.3), channel_id=1, source_target_pairs={{0,4},{4,8},{8,12},{12,16},{16,20},{20,24},{24,28},{28,0},{1,5},{5... | collective-permute-start | bytes 786440 | tf_op jit(solution)/shard_map/ppermute | solution.py:35
  35.1 6.7 %collective-permute-start.5 = (bf16[512,256]{1,0:T(8,128)(2,1)S(1)}, bf16[512,256]{1,0:T(8,128)(2,1)S(1)}, u32[]{:S(2)}, u32[]{:S(2)}) collective-permute-start(bf16[512,256]{1,0:T(8,128)(2,1)S(1)} %collective-permute-done.4), channel_id=1, source_target_pairs={{0,4},{4,8},{8,12},{12,16},{16,20},{20,24},{24,28},{28,0},{1,5},{5... | collective-permute-start | bytes 786440 | tf_op jit(solution)/shard_map/ppermute | solution.py:35
  41.8 6.7 %collective-permute-start.6 = (bf16[512,256]{1,0:T(8,128)(2,1)S(1)}, bf16[512,256]{1,0:T(8,128)(2,1)S(1)}, u32[]{:S(2)}, u32[]{:S(2)}) collective-permute-start(bf16[512,256]{1,0:T(8,128)(2,1)S(1)} %collective-permute-done.5), channel_id=1, source_target_pairs={{0,4},{4,8},{8,12},{12,16},{16,20},{20,24},{24,28},{28,0},{1,5},{5... | collective-permute-start | bytes 786440 | tf_op jit(solution)/shard_map/ppermute | solution.py:35
  48.7 1.0 copy-start.1
  48.7 1.0 copy-start.3
  212.8 0.6 copy-start.2
